TPU v7x, 256 devices: a whole 4x4x8 slice. The times are simulated.
256 devices in a mesh: dp: 32 (over z_hi, x, y), tensor: 8 (over z_lo, core).
Axes of the slice: x: 4, y: 4, z: 8 (z_hi: 2, z_lo: 4; z = z_hi * 4 + z_lo), core: 2. Of those that a mesh axis runs over, the one named last changes fastest.
Arguments:
- tokens: bfloat16 [8192, 4096], P(('dp', 'tensor')), may hold values from -6 to 6
- out_grad: bfloat16 [8192, 4096], P(('dp', 'tensor')), may hold values from -6 to 6
- weight_tiles: bfloat16 [128, 3, 112, 3, 128], P('dp', None, 'tensor'), may hold values from -0.3125 to 0.3125
- tile_counts: int32 [3, 112], P(None, 'tensor'), may hold values from 1 to 3, as said below
- tile_rows: int32 [3, 112, 3], P(None, 'tensor'), may hold values from 0 to 31, as said below
Outputs:
- ffn_out: bfloat16 [8192, 4096], P(('dp', 'tensor'))
- input_grad: bfloat16 [8192, 4096], P(('dp', 'tensor'))
- tile_grad: bfloat16 [128, 3, 112, 3, 128], P('dp', None, 'tensor')
Inputs may be any that keep to these rules, and one draw needn't show every extreme that they name: `tile_counts`: for each matrix and each q, the live slots of hidden blocks q * 14 to (q + 1) * 14 - 1 number at most 28 together, and for each matrix some q reaches 28. `tile_rows`: within one hidden block of one matrix the 3 feature blocks are distinct.
All inputs are finite; a program needn't handle non-finite values.
Results may differ from a plain program's by a relative error of at most 0.018.
Values may be sent and summed in bfloat16 or wider, within the bound.
A program may use at most 128 MiB of HBM per device.

v0:
```python
import math

import jax
import jax.numpy as jnp
from jax import lax
from jax.sharding import PartitionSpec as P


def shards(tokens, out_grad, weight_tiles, tile_counts, tile_rows):
    highest = lax.Precision.HIGHEST
    row_share = weight_tiles.shape[0]
    blocks_dev = weight_tiles.shape[2]
    slot_count = weight_tiles.shape[3]
    tile_size = weight_tiles.shape[4]
    feature_count = tokens.shape[1]
    row_blocks = feature_count // tile_size
    slot_total = blocks_dev * slot_count
    own_rows = tokens.shape[0]
    grad_scale = 1.0 / math.sqrt(own_rows * lax.axis_size("tensor") * lax.axis_size("dp"))
    inputs, grads_in = (
        lax.all_gather(tokens, "tensor", axis=0, tiled=True),
        lax.all_gather(out_grad, "tensor", axis=0, tiled=True),
    )
    group_rows = inputs.shape[0]
    live_all = (
        jnp.arange(slot_count, dtype=jnp.int32)[None, None, :] < tile_counts[:, :, None]
    ).reshape(3, slot_total)
    rows_all = tile_rows.reshape(3, slot_total)
    cols_all = jnp.broadcast_to(
        jnp.repeat(jnp.arange(blocks_dev, dtype=jnp.int32), slot_count)[None, :], (3, slot_total)
    )
    own_tiles = weight_tiles.reshape(row_share, 3, slot_total, tile_size)
    weights = lax.all_gather(own_tiles, "dp", axis=0, tiled=True)
    live_mask = live_all.astype(jnp.float32)
    col_onehot = (
        cols_all[:, :, None] == jnp.arange(blocks_dev, dtype=jnp.int32)[None, None, :]
    ).astype(jnp.float32) * live_mask[:, :, None]
    row_onehot = (
        rows_all[:, :, None] == jnp.arange(row_blocks, dtype=jnp.int32)[None, None, :]
    ).astype(jnp.float32) * live_mask[:, :, None]
    input_blocks = inputs.reshape(group_rows, row_blocks, tile_size)
    grad_blocks = grads_in.reshape(group_rows, row_blocks, tile_size)
    gate_sel = jnp.take(input_blocks, rows_all[0], axis=1)
    up_sel = jnp.take(input_blocks, rows_all[1], axis=1)
    gate_prod = jnp.einsum(
        "tsa,asb->tsb", gate_sel, weights[:, 0], preferred_element_type=jnp.float32
    )
    gate_pre = jnp.einsum("tsb,sj->tjb", gate_prod, col_onehot[0], precision=highest)
    up_prod = jnp.einsum("tsa,asb->tsb", up_sel, weights[:, 1], preferred_element_type=jnp.float32)
    up_pre = jnp.einsum("tsb,sj->tjb", up_prod, col_onehot[1], precision=highest)
    gate_sig = jax.nn.sigmoid(gate_pre)
    gate_act = gate_pre * gate_sig
    hidden = (gate_act * up_pre).astype(jnp.bfloat16)
    hidden_sel = jnp.take(hidden, cols_all[2], axis=1)
    products = jnp.einsum(
        "tsa,asb->tsb", hidden_sel, weights[:, 2], preferred_element_type=jnp.float32
    )
    ffn_rows = lax.psum_scatter(
        jnp.einsum("tsb,sr->trb", products, row_onehot[2], precision=highest)
        .reshape(lax.axis_size("tensor") * own_rows, feature_count)
        .astype(jnp.bfloat16),
        "tensor",
        scatter_dimension=0,
        tiled=True,
    )
    grad_sel = jnp.take(grad_blocks, rows_all[2], axis=1)
    dh_slots = jnp.einsum(
        "tsb,asb->tsa", grad_sel, weights[:, 2], preferred_element_type=jnp.float32
    )
    dh_blocks = jnp.einsum("tsa,sj->tja", dh_slots, col_onehot[2], precision=highest)
    grad_gate = (dh_blocks * up_pre * gate_sig * (1.0 + gate_pre * (1.0 - gate_sig))).astype(
        jnp.bfloat16
    )
    grad_up = (dh_blocks * gate_act).astype(jnp.bfloat16)
    dgate_sel = jnp.take(grad_gate, cols_all[0], axis=1)
    dup_sel = jnp.take(grad_up, cols_all[1], axis=1)
    tile_terms = jnp.stack(
        [
            jnp.einsum("tsa,tsb->asb", gate_sel, dgate_sel, preferred_element_type=jnp.float32),
            jnp.einsum("tsa,tsb->asb", up_sel, dup_sel, preferred_element_type=jnp.float32),
            jnp.einsum("tsa,tsb->asb", hidden_sel, grad_sel, preferred_element_type=jnp.float32),
        ],
        axis=1,
    )
    tile_sums = lax.psum_scatter(
        (tile_terms * (live_mask * grad_scale)[None, :, :, None]).astype(jnp.bfloat16),
        "dp",
        scatter_dimension=0,
        tiled=True,
    ).astype(jnp.float32)
    from_gate = jnp.einsum(
        "tsb,asb->tsa", dgate_sel, weights[:, 0], preferred_element_type=jnp.float32
    )
    from_up = jnp.einsum("tsb,asb->tsa", dup_sel, weights[:, 1], preferred_element_type=jnp.float32)
    summed = jnp.einsum("tsa,sr->tra", from_gate, row_onehot[0], precision=highest)
    summed = summed + jnp.einsum("tsa,sr->tra", from_up, row_onehot[1], precision=highest)
    input_rows = lax.psum_scatter(
        summed.reshape(lax.axis_size("tensor") * own_rows, feature_count).astype(jnp.bfloat16),
        "tensor",
        scatter_dimension=0,
        tiled=True,
    )
    tile_grad = tile_sums.reshape(row_share, 3, blocks_dev, slot_count, tile_size).astype(
        jnp.bfloat16
    )
    return (ffn_rows, input_rows, tile_grad)


def solution(mesh):
    return jax.shard_map(
        shards,
        mesh=mesh,
        in_specs=(
            P(("dp", "tensor"), None),
            P(("dp", "tensor"), None),
            P("dp", None, "tensor", None, None),
            P(None, "tensor"),
            P(None, "tensor", None),
        ),
        out_specs=(
            P(("dp", "tensor"), None),
            P(("dp", "tensor"), None),
            P("dp", None, "tensor", None, None),
        ),
        check_vma=False,
    )
```

profile of v0, /device:TPU:24, one launch (start us, length us, event | category | flops | bytes accessed | tf_op | source)
XLA Modules:
  0.0 620.1 jit_solution(10170199385363920965)
XLA Ops:
  12.9 38.4 %all-gather.8.cloned.1.call-done = bf16[256,4096]{1,0:T(8,128)(2,1)} async-done(((bf16[32,4096]{1,0:T(8,128)(2,1)}), bf16[256,4096]{1,0:T(8,128)(2,1)}) %all-gather.8.cloned.1.call-update) | async-done | bytes 2097168 | tf_op jit(solution)/shard_map/all_gather | solution.py:22
  51.3 3.3 copy.119
  54.5 2.9 copy.120
  57.5 33.9 %all-gather.4.cloned.1.call-done = bf16[256,4096]{1,0:T(8,128)(2,1)} async-done(((bf16[32,4096]{1,0:T(8,128)(2,1)}), bf16[256,4096]{1,0:T(8,128)(2,1)}) %all-gather.4.cloned.1.call-update) | async-done | bytes 2097168 | tf_op jit(solution)/shard_map/all_gather | solution.py:21
  91.3 4.1 copy.105
  95.4 3.2 copy.106
  98.6 2.6 gather_fusion
  101.2 2.7 gather_fusion.1
  103.9 2.7 gather_fusion.3
  106.6 103.2 %all-gather.6.cloned.1.call-done = bf16[128,3,42,128]{3,2,1,0:T(8,128)(2,1)} async-done(((bf16[4,3,42,128]{3,2,1,0:T(8,128)(2,1)}), bf16[128,3,42,128]{3,2,1,0:T(8,128)(2,1)}) %all-gather.6.cloned.1.call-update) | async-done | bytes 4128784 | tf_op jit(solution)/shard_map/all_gather | solution.py:33
  209.8 3.2 fusion.92
  215.1 6.0 fusion.5
  222.1 6.2 %fusion.11 = f32[14,256,128]{2,0,1:T(8,128)S(1)} fusion(f32[256,42,128]{2,0,1:T(8,128)S(1)} %fusion.34, f32[3,42,14]{1,2,0:T(8,128)S(1)} %fusion.82), kind=kOutput, calls=%fused_computation.18 | convolution fusion | flops 231211008 | bytes 7348224 | tf_op jit(solution)/shard_map/tsb,sj->tjb/dot_general | solution.py:48
  229.3 6.4 %fusion.9 = f32[14,256,128]{2,0,1:T(8,128)S(1)} fusion(f32[256,42,128]{2,0,1:T(8,128)S(1)} %fusion.37, f32[3,42,14]{1,2,0:T(8,128)S(1)} %fusion.82), kind=kOutput, calls=%fused_computation.16 | convolution fusion | flops 231211008 | bytes 7348224 | tf_op jit(solution)/shard_map/tsb,sj->tjb/dot_general | solution.py:50
  237.9 2.6 gather_fusion.2
  240.4 2.6 gather_fusion.4
  243.1 5.4 fusion.66
  248.5 2.7 fusion.71
  251.2 2.6 gather_fusion.5
  253.8 3.9 fusion.76
  258.0 2.4 fusion
  260.4 7.0 %copy.128 = bf16[128,3,42,128]{3,2,1,0:T(8,128)(2,1)} copy(bf16[128,3,42,128]{0,3,2,1:T(8,128)(2,1)} %fusion) | data formatting | bytes 8257536 | tf_op jit(solution)/shard_map/convert_element_type | solution.py:86
  269.2 2.5 fusion.49
  272.9 7.1 %fusion.1 = f32[32,256,128]{2,0,1:T(8,128)S(1)} fusion(f32[256,42,128]{2,0,1:T(8,128)S(1)} %fusion.49, f32[3,42,32]{1,2,0:T(8,128)S(1)} %fusion.81), kind=kOutput, calls=%fused_computation.8 | convolution fusion | flops 528482304 | bytes 9715712 | tf_op jit(solution)/shard_map/tsa,sr->tra/dot_general | solution.py:96
  280.0 10.1 %add_convert_fusion = bf16[32,256,128]{2,0,1:T(8,128)(2,1)S(1)} fusion(f32[32,256,128]{2,0,1:T(8,128)S(1)} %fusion.1, f32[256,42,128]{2,0,1:T(8,128)S(1)} %fusion.46, f32[3,42,32]{1,2,0:T(8,128)S(1)} %fusion.81), kind=kOutput, calls=%fused_computation.20 | convolution fusion | flops 530579456 | bytes 11812864 | tf_op jit(solution)/shard_map/tsa,sr->tra/dot_general | solution.py:95
  290.1 2.4 copy.175
  292.6 2.4 fusion.40
  295.0 10.0 %fusion.54 = bf16[32,256,128]{2,0,1:T(8,128)(2,1)S(1)} fusion(f32[256,42,128]{2,0,1:T(8,128)S(1)} %fusion.40, f32[3,42,32]{1,2,0:T(8,128)S(1)} %fusion.81), kind=kOutput, calls=%fused_computation.56 | convolution fusion | flops 529530880 | bytes 7618560 | tf_op jit(solution)/shard_map/tsb,sr->trb/dot_general | solution.py:59
  305.0 2.4 copy.176
  307.4 221.0 %reduce-scatter.8.cloned.1.call-done = bf16[4,3,42,128]{3,2,1,0:T(8,128)(2,1)} async-done(((bf16[128,3,42,128]{3,2,1,0:T(8,128)(2,1)}), bf16[4,3,42,128]{3,2,1,0:T(8,128)(2,1)}) %reduce-scatter.8.cloned.1.call-update) | async-done | bytes 129040 | tf_op jit(solution)/shard_map/reduce_scatter | solution.py:85
  530.0 39.5 %reduce-scatter.6.cloned.1.call-done = bf16[32,4096]{1,0:T(8,128)(2,1)} async-done(((bf16[256,4096]{1,0:T(8,128)(2,1)}), bf16[32,4096]{1,0:T(8,128)(2,1)}) %reduce-scatter.6.cloned.1.call-update) | async-done | bytes 262160 | tf_op jit(solution)/shard_map/reduce_scatter | solution.py:97
  569.4 43.4 %reduce-scatter.4.cloned.1.call-done = bf16[32,4096]{1,0:T(8,128)(2,1)} async-done(((bf16[256,4096]{1,0:T(8,128)(2,1)}), bf16[32,4096]{1,0:T(8,128)(2,1)}) %reduce-scatter.4.cloned.1.call-update) | async-done | bytes 262160 | tf_op jit(solution)/shard_map/reduce_scatter | solution.py:58
  (79 shorter events, 16.5 us)
Async XLA Ops:
  7.2 44.1 %all-gather.8.cloned.1.call-start = ((), (), s32[]{:S(2)}) async-start(), calls=%async_computation.6 | async-start | bytes 2359296 | tf_op jit(solution)/shard_map/all_gather | solution.py:22
  7.9 83.4 %all-gather.4.cloned.1.call-start = ((), (), s32[]{:S(2)}) async-start(), calls=%async_computation.3 | async-start | bytes 2359296 | tf_op jit(solution)/shard_map/all_gather | solution.py:21
  8.6 201.1 %all-gather.6.cloned.1.call-start = ((), (), s32[]{:S(2)}) async-start(), calls=%async_computation.4 | async-start | bytes 4866048 | tf_op jit(solution)/shard_map/all_gather | solution.py:33
  10.3 518.1 %reduce-scatter.8.cloned.1.call-start = ((), (), s32[]{:S(2)}) async-start(), calls=%async_computation.8 | async-start | bytes 4866048 | tf_op jit(solution)/shard_map/reduce_scatter | solution.py:85
  106.5 106.5 %copy-start.6 = (bf16[42,256,128]{2,1,0:T(8,128)(2,1)}, bf16[42,256,128]{2,1,0:T(8,128)(2,1)S(1)}, u32[]{:S(2)}) copy-start(bf16[42,256,128]{2,1,0:T(8,128)(2,1)S(1)} %gather_fusion.3) | copy-start | bytes 8257540
  213.0 1.2 copy-start.8
  213.0 8.2 %copy-start.9 = (bf16[128,1,42,128]{3,2,1,0:T(8,128)(2,1)}, bf16[128,1,42,128]{3,2,1,0:T(8,128)(2,1)S(1)}, u32[]{:S(2)}) copy-start(bf16[128,1,42,128]{3,2,1,0:T(8,128)(2,1)S(1)} %get-tuple-element.21) | copy-start | bytes 4128772
  213.0 15.4 %copy-start.11 = (bf16[128,1,42,128]{3,2,1,0:T(8,128)(2,1)}, bf16[128,1,42,128]{3,2,1,0:T(8,128)(2,1)S(1)}, u32[]{:S(2)}) copy-start(bf16[128,1,42,128]{3,2,1,0:T(8,128)(2,1)S(1)} %get-tuple-element.20) | copy-start | bytes 4128772
  215.1 6.1 copy-start.2
  222.1 6.3 %copy-start.1 = (bf16[42,256,128]{2,1,0:T(8,128)(2,1)S(1)}, bf16[42,256,128]{2,1,0:T(8,128)(2,1)}, u32[]{:S(2)}) copy-start(bf16[42,256,128]{2,1,0:T(8,128)(2,1)} %gather_fusion.1) | copy-start | bytes 8257540
  243.1 5.4 copy-start.3
  243.1 5.4 copy-start.4
  253.8 3.9 copy-start.12
  253.8 4.2 copy-start.13
  267.4 0.7 copy-start.14
  267.4 1.8 copy-start.7
  267.4 302.0 %reduce-scatter.6.cloned.1.call-start = ((), (), s32[]{:S(2)}) async-start(), calls=%async_computation.7 | async-start | bytes 2359296 | tf_op jit(solution)/shard_map/reduce_scatter | solution.py:97
  269.2 2.5 copy-start.5
  269.2 2.7 copy-start.10
  290.1 2.5 copy-start
  292.5 320.3 %reduce-scatter.4.cloned.1.call-start = ((), (), s32[]{:S(2)}) async-start(), calls=%async_computation.5 | async-start | bytes 2359296 | tf_op jit(solution)/shard_map/reduce_scatter | solution.py:58
Sparse Core Ops, SparseCore 0:
  9.8 41.4 all-gather.7
  53.1 38.2 all-gather.3
  95.4 114.3 all-gather.5
  267.6 260.7 reduce-scatter.7
  531.3 38.0 reduce-scatter.5
  572.4 40.3 reduce-scatter.3
where the time goes:
time: 631 us; the launch traced here: 620 us
  waiting for transfers between devices  481 us (76%)
  matrix products  66.5 us (11%)
  local copies, waits for them, and re-layouts  52.8 us (8%)
  between operations  15 us (2%)
    reduce_scatter x1, waiting for transfers between devices, shards(): lax.psum_scatter((tile_terms * (live_mask * grad_scale)[None, :, :, None]...  221 us
    all_gather x1, waiting for transfers between devices, shards(): weights = lax.all_gather(own_tiles, 'dp', axis=0, tiled=True)  103 us
    reduce_scatter x1, waiting for transfers between devices, shards(): lax.psum_scatter(jnp.einsum('tsb,sr->trb', products, row_onehot[2], preci...  43.4 us
    reduce_scatter x1, waiting for transfers between devices, shards(): lax.psum_scatter(summed.reshape(lax.axis_size('tensor') * own_rows, featu...  39.5 us
    all_gather x1, waiting for transfers between devices, shards(): lax.all_gather(out_grad, 'tensor', axis=0, tiled=True)  38.4 us
    all_gather x1, waiting for transfers between devices, shards(): lax.all_gather(tokens, 'tensor', axis=0, tiled=True)  33.9 us
  transfers between devices with their start and end apart: 6, of which 6 were waited for; matrix products, arithmetic and copies ran while one was open for 10% of the time, Pallas kernels for 0%

commit v1 on v0

v1 whole, which is shorter than its diff:
```python
import functools
import math

import jax
import jax.numpy as jnp
from jax import lax
from jax.experimental import pallas as pl
from jax.experimental.pallas import tpu as pltpu
from jax.sharding import PartitionSpec as P

MESH = pl.DeviceIdType.MESH
BF = jnp.bfloat16
F32 = jnp.float32
ANY = pl.BlockSpec(memory_space=pl.ANY)
VM = pl.BlockSpec(memory_space=pltpu.VMEM)
SM = pl.BlockSpec(memory_space=pltpu.SMEM)

CAP = 28
SLOTS = 3 * CAP
HALF = SLOTS // 2
BLOCKS = 14
ROWS = 32
WIDTH = 4096
TILE = 128


def places():
    d = lax.axis_index("dp")
    t = lax.axis_index("tensor")
    return d // 16, (d // 4) % 4, d % 4, t // 2, t % 2


def piece_at(zh, x, y):
    return zh * 16 + x * 4 + y


def greet(zh, x, y, z, c):
    barrier = pltpu.get_barrier_semaphore()
    peers = [
        {"tensor": ((z + 1) % 4) * 2 + c},
        {"tensor": ((z + 3) % 4) * 2 + c},
        {"tensor": z * 2 + 1 - c},
        {"dp": piece_at(zh, x, (y + 1) % 4)},
        {"dp": piece_at(zh, x, (y + 3) % 4)},
        {"dp": piece_at(zh, (x + 1) % 4, y)},
        {"dp": piece_at(zh, (x + 3) % 4, y)},
        {"dp": piece_at(1 - zh, x, y)},
    ]
    for peer in peers:
        pl.semaphore_signal(barrier, inc=1, device_id=peer, device_id_type=MESH)
    pl.semaphore_wait(barrier, len(peers))


def gather_kernel(
    counts, x_in, g_in, w_in, x_out, g_out, w_out, w_own, xs_send, xs_recv, w_send, w_recv, local
):
    zh, x, y, z, c = places()
    t = z * 2 + c
    ins, outs = (x_in, g_in), (x_out, g_out)
    greet(zh, x, y, z, c)

    def rows_of(arr, shard):
        return outs[arr].at[pl.ds(pl.multiple_of(shard * ROWS, ROWS), ROWS)]

    def act_copy(arr, shard, way, src, peer):
        return pltpu.make_async_remote_copy(
            src_ref=src,
            dst_ref=rows_of(arr, shard),
            send_sem=xs_send.at[arr, shard, way],
            recv_sem=xs_recv.at[arr, shard],
            device_id={"tensor": peer},
            device_id_type=MESH,
        )

    right, left, mate = t + 2, t - 2, z * 2 + 1 - c

    def to(arr, shard, way, src):
        return act_copy(arr, shard, way, src, (right, left, mate)[way])

    def compact(m):
        def step(i, carry):
            j, k = carry
            w_own[m * CAP + i] = w_in[m * 42 + j * 3 + k]
            more = k + 1 < counts[m, j]
            return (
                jnp.where(more, j, jnp.minimum(j + 1, BLOCKS - 1)),
                jnp.where(more, k + 1, 0),
            )

        lax.fori_loop(0, CAP, step, (jnp.int32(0), jnp.int32(0)))

    for m in range(3):
        compact(m)

    me = piece_at(zh, x, y)
    halves = (pl.ds(0, HALF), pl.ds(HALF, HALF))

    def w_part(piece, half):
        if half is None:
            return w_out.at[:, piece]
        return w_out.at[halves[half], piece]

    def w_copy(piece, half, way, peer, src=None):
        return pltpu.make_async_remote_copy(
            src_ref=w_part(piece, half) if src is None else src,
            dst_ref=w_part(piece, half),
            send_sem=w_send.at[piece, way],
            recv_sem=w_recv.at[piece, 1 if half == 1 else 0],
            device_id={"dp": peer},
            device_id_type=MESH,
        )

    xp, xm = piece_at(zh, (x + 1) % 4, y), piece_at(zh, (x + 3) % 4, y)
    yp, ym = piece_at(zh, x, (y + 1) % 4), piece_at(zh, x, (y + 3) % 4)
    zo = piece_at(1 - zh, x, y)

    w_copy(me, None, 6, zo, w_own).start()
    w_copy(me, None, 2, yp, w_own).start()
    w_copy(me, None, 3, ym, w_own).start()
    w_copy(me, None, 0, xp, w_own).start()
    w_copy(me, None, 1, xm, w_own).start()
    for arr in range(2):

        @pl.when(z < 3)
        def _():
            to(arr, t, 0, ins[arr]).start()

        @pl.when(z > 0)
        def _():
            to(arr, t, 1, ins[arr]).start()

        to(arr, t, 2, ins[arr]).start()
    own_copies = [
        pltpu.make_async_copy(x_in, rows_of(0, t), local.at[0]),
        pltpu.make_async_copy(g_in, rows_of(1, t), local.at[1]),
        pltpu.make_async_copy(w_own, w_out.at[:, me], local.at[2]),
    ]
    for copy in own_copies:
        copy.start()

    def along_y(h):
        base = h * 16 + x * 4
        near, far, opp = base + (y + 3) % 4, base + (y + 1) % 4, base + (y + 2) % 4
        w_copy(near, None, 0, me).wait_recv()
        w_copy(near, 0, 2, yp).start()
        w_copy(near, None, 0, xp).start()
        w_copy(near, None, 1, xm).start()
        w_copy(far, None, 0, me).wait_recv()
        w_copy(far, 1, 3, ym).start()
        w_copy(far, None, 0, xp).start()
        w_copy(far, None, 1, xm).start()
        w_copy(opp, 0, 0, me).wait_recv()
        w_copy(opp, 1, 0, me).wait_recv()
        w_copy(opp, None, 0, xp).start()
        w_copy(opp, None, 1, xm).start()

    def along_x(h):
        for dy in (0, 3, 1, 2):
            yy = (y + dy) % 4
            near = h * 16 + ((x + 3) % 4) * 4 + yy
            far = h * 16 + ((x + 1) % 4) * 4 + yy
            w_copy(near, None, 0, me).wait_recv()
            w_copy(near, 0, 4, xp).start()
            w_copy(far, None, 0, me).wait_recv()
            w_copy(far, 1, 5, xm).start()

    def along_z(n, arr):
        @pl.when(z - n >= 0)
        def _():
            shard = t - 2 * n
            act_copy(arr, shard, 0, rows_of(arr, shard), t).wait_recv()

            @pl.when(z < 3)
            def _():
                to(arr, shard, 0, rows_of(arr, shard)).start()

            to(arr, shard, 2, rows_of(arr, shard)).start()

        @pl.when(z + n <= 3)
        def _():
            shard = t + 2 * n
            act_copy(arr, shard, 0, rows_of(arr, shard), t).wait_recv()

            @pl.when(z > 0)
            def _():
                to(arr, shard, 1, rows_of(arr, shard)).start()

            to(arr, shard, 2, rows_of(arr, shard)).start()

    along_y(zh)
    zpiece = zo
    w_copy(zpiece, None, 0, me).wait_recv()
    w_copy(zpiece, None, 2, yp).start()
    w_copy(zpiece, None, 3, ym).start()
    w_copy(zpiece, None, 0, xp).start()
    w_copy(zpiece, None, 1, xm).start()
    along_z(1, 0)
    along_y(1 - zh)
    along_z(1, 1)
    along_x(zh)
    along_z(2, 0)
    along_x(1 - zh)
    along_z(2, 1)
    along_z(3, 0)
    along_z(3, 1)

    for zz in range(4):
        for arr in range(2):
            act_copy(arr, zz * 2 + 1 - c, 0, rows_of(arr, zz * 2 + 1 - c), t).wait_recv()
    for h in range(2):
        for yy in range(4):
            opp = h * 16 + ((x + 2) % 4) * 4 + yy
            w_copy(opp, 0, 0, me).wait_recv()
            w_copy(opp, 1, 0, me).wait_recv()
    for copy in own_copies:
        copy.wait()

    for arr in range(2):
        for zz in range(4):
            shard = zz * 2 + c

            @pl.when((zz <= z) & (z < 3))
            def _():
                to(arr, shard, 0, ins[arr]).wait_send()

            @pl.when((zz >= z) & (z > 0))
            def _():
                to(arr, shard, 1, ins[arr]).wait_send()

            to(arr, shard, 2, ins[arr]).wait_send()
    w_copy(me, None, 6, zo, w_own).wait_send()
    for h in range(2):
        base = h * 16 + x * 4
        for dy in range(4):
            yy = (y + dy) % 4
            w_copy(base + yy, None, 0, xp).wait_send()
            w_copy(base + yy, None, 1, xm).wait_send()
            w_copy(h * 16 + ((x + 3) % 4) * 4 + yy, 0, 4, xp).wait_send()
            w_copy(h * 16 + ((x + 1) % 4) * 4 + yy, 1, 5, xm).wait_send()
        w_copy(base + y, None, 2, yp).wait_send()
        w_copy(base + y, None, 3, ym).wait_send()
        w_copy(base + (y + 3) % 4, 0, 2, yp).wait_send()
        w_copy(base + (y + 1) % 4, 1, 3, ym).wait_send()


def gather(counts, tokens, out_grad, tiles):
    return pl.pallas_call(
        gather_kernel,
        name="gather",
        out_shape=(
            jax.ShapeDtypeStruct((8 * ROWS, WIDTH), BF),
            jax.ShapeDtypeStruct((8 * ROWS, WIDTH), BF),
            jax.ShapeDtypeStruct((SLOTS, 32, 4, TILE), BF),
        ),
        in_specs=[SM, ANY, ANY, VM],
        out_specs=(ANY, ANY, ANY),
        scratch_shapes=[
            pltpu.VMEM((SLOTS, 4, TILE), BF),
            pltpu.SemaphoreType.DMA((2, 8, 3)),
            pltpu.SemaphoreType.DMA((2, 8)),
            pltpu.SemaphoreType.DMA((32, 7)),
            pltpu.SemaphoreType.DMA((32, 2)),
            pltpu.SemaphoreType.DMA((3,)),
        ],
        compiler_params=pltpu.CompilerParams(collective_id=0, has_side_effects=True),
    )(counts, tokens, out_grad, tiles)


def dot(a, b, dims):
    return lax.dot_general(a, b, (dims, ((), ())), preferred_element_type=F32)


def block_kernel(scale, counts, rows, x, g, w, f_out, i_out, tg, acc_f, acc_i):
    acc_f[...] = jnp.zeros_like(acc_f)
    acc_i[...] = jnp.zeros_like(acc_i)

    def column(ref, r):
        return ref.at[:, pl.ds(pl.multiple_of(r * TILE, TILE), TILE)]

    def step(j, offsets):
        tiles, blocks, live, where = [], [], [], []
        for m in range(3):
            n = counts[m, j]
            src = x if m < 2 else g
            tiles.append([])
            blocks.append([])
            live.append([])
            where.append([])
            for k in range(3):
                on = k < n
                r = rows[m * 3 + k, j]
                at = m * CAP + offsets[m] + k
                tile = w[jnp.minimum(at, SLOTS - 1)]
                if k:
                    tile = jnp.where(on, tile, jnp.zeros_like(tile))
                tiles[m].append(tile)
                blocks[m].append(column(src, r)[...])
                live[m].append(on)
                where[m].append((r, at))
        x0 = jnp.concatenate(blocks[0], axis=1)
        x1 = jnp.concatenate(blocks[1], axis=1)
        g2 = jnp.concatenate(blocks[2], axis=1)
        w0 = jnp.concatenate(tiles[0], axis=0)
        w1 = jnp.concatenate(tiles[1], axis=0)
        w2 = jnp.concatenate(tiles[2], axis=1)
        gate = dot(x0, w0, ((1,), (0,)))
        up = dot(x1, w1, ((1,), (0,)))
        dh = dot(g2, w2, ((1,), (1,)))
        sig = jax.nn.sigmoid(gate)
        act = gate * sig
        hidden = (act * up).astype(BF)
        d_gate = (dh * up * sig * (1.0 + gate * (1.0 - sig))).astype(BF)
        d_up = (dh * act).astype(BF)
        for m, (value, acc) in enumerate(((d_gate, acc_i), (d_up, acc_i), (hidden, acc_f))):
            wide = dot(value, (w0, w1, w2)[m], ((1,), (1 if m < 2 else 0,)))
            if m < 2:
                terms = dot((x0, x1)[m], value, ((0,), (0,))) * scale
            else:
                terms = dot(value, g2, ((0,), (0,))) * scale
            for k in range(3):
                r, at = where[m][k]

                def put():
                    column(acc, r)[...] += wide[:, k * TILE : (k + 1) * TILE]
                    part = (
                        terms[k * TILE : (k + 1) * TILE]
                        if m < 2
                        else terms[:, k * TILE : (k + 1) * TILE]
                    )
                    tg[at] = part.astype(BF)

                if k:
                    pl.when(live[m][k])(put)
                else:
                    put()
        return tuple(offsets[m] + counts[m, j] for m in range(3))

    lax.fori_loop(0, BLOCKS, step, (jnp.int32(0),) * 3)
    f_out[...] = acc_f[...].astype(BF)
    i_out[...] = acc_i[...].astype(BF)


def compute(counts, rows, x, g, w, scale):
    return pl.pallas_call(
        functools.partial(block_kernel, scale),
        name="blocks",
        out_shape=(
            jax.ShapeDtypeStruct(x.shape, BF),
            jax.ShapeDtypeStruct(x.shape, BF),
            jax.ShapeDtypeStruct((SLOTS, TILE, TILE), BF),
        ),
        in_specs=[SM, SM, VM, VM, VM],
        out_specs=(VM, VM, VM),
        scratch_shapes=[pltpu.VMEM(x.shape, F32), pltpu.VMEM(x.shape, F32)],
        compiler_params=pltpu.CompilerParams(vmem_limit_bytes=56 * 1024 * 1024),
    )(counts, rows, x, g, w)


def scatter_kernel(
    counts,
    f_in,
    i_in,
    tg,
    f_out,
    i_out,
    w_out,
    own,
    mate_in,
    from_left,
    from_right,
    total,
    tx0,
    tx1,
    tx2,
    xa,
    xb,
    xs_lo,
    xs_hi,
    xl,
    xr,
    yb,
    ya,
    yc,
    ys_lo,
    ys_hi,
    yl,
    yr,
    z_own,
    z_send,
    z_in,
    z_sum,
    act_local,
    act_mate_s,
    act_mate_r,
    act_send,
    act_left,
    act_right,
    x_local,
    x_send,
    x_recv,
    y_send,
    y_recv,
    z_sems,
):
    zh, x, y, z, c = places()
    t = z * 2 + c
    ins, outs = (f_in, i_in), (f_out, i_out)
    greet(zh, x, y, z, c)
    lo, hi = pl.ds(0, HALF), pl.ds(HALF, HALF)
    xp, xm = piece_at(zh, (x + 1) % 4, y), piece_at(zh, (x + 3) % 4, y)
    yp, ym = piece_at(zh, x, (y + 1) % 4), piece_at(zh, x, (y + 3) % 4)
    zo = piece_at(1 - zh, x, y)

    def remote(src, dst, send, recv, peer):
        return pltpu.make_async_remote_copy(
            src_ref=src,
            dst_ref=dst,
            send_sem=send,
            recv_sem=recv,
            device_id=peer,
            device_id_type=MESH,
        )

    def rows_of(arr, shard):
        return ins[arr].at[pl.ds(pl.multiple_of(shard * ROWS, ROWS), ROWS)]

    def mate_copy(arr, zz):
        return remote(
            rows_of(arr, zz * 2 + 1 - c),
            mate_in.at[arr, zz],
            act_mate_s.at[arr, zz],
            act_mate_r.at[arr, zz],
            {"tensor": z * 2 + 1 - c},
        )

    def own_copy(arr, zz):
        return pltpu.make_async_copy(
            rows_of(arr, zz * 2 + c), own.at[arr, zz], act_local.at[arr, zz]
        )

    def tx_copy(n):
        return pltpu.make_async_copy(tg.at[:, :, (x + (3, 1, 0)[n]) % 4], (tx0, tx1, tx2)[n], x_local.at[n])

    px, mx = {"dp": xp}, {"dp": xm}
    opp, fwd, bwd = (x + 2) % 4, (x + 1) % 4, (x + 3) % 4
    x_copies = [
        remote(tg.at[lo, :, opp], xa, x_send.at[0], x_recv.at[0], px),
        remote(tg.at[hi, :, opp], xb, x_send.at[1], x_recv.at[1], mx),
        remote(tg.at[hi, :, fwd], xl.at[hi], x_send.at[2], x_recv.at[2], px),
        remote(tg.at[lo, :, bwd], xr.at[lo], x_send.at[3], x_recv.at[3], mx),
        remote(xs_lo, xl.at[lo], x_send.at[4], x_recv.at[4], px),
        remote(xs_hi, xr.at[hi], x_send.at[5], x_recv.at[5], mx),
    ]
    for n in range(4):
        x_copies[n].start()
    order = ((0, 3), (0, 0), (1, 3), (1, 0), (0, 2), (0, 1), (1, 2), (1, 1))
    for arr, zz in order:
        mate_copy(arr, zz).start()
        own_copy(arr, zz).start()
    for n in range(3):
        tx_copy(n).start()

    def along(arr, zz, buf, sems, way, has):
        own_copy(arr, zz).wait()
        mate_copy(arr, zz).wait_recv()

        @pl.when(has)
        def _():
            remote(
                total.at[arr, zz], buf.at[arr, zz], act_send.at[arr, zz], sems.at[arr, zz],
                {"tensor": t},
            ).wait_recv()
            chunks(total, (own, mate_in, buf), arr, zz)

        @pl.when(jnp.logical_not(has))
        def _():
            chunks(total, (own, mate_in), arr, zz)

        remote(
            total.at[arr, zz], buf.at[arr, zz], act_send.at[arr, zz], sems.at[arr, zz],
            {"tensor": t + way},
        ).start()

    def chunks(dst, srcs, *lead):
        for n in range(0, WIDTH, 512):
            s = pl.ds(n, 512)
            at = (*lead, slice(None), s)
            acc = srcs[0][at].astype(F32)
            for src in srcs[1:]:
                acc = acc + src[at].astype(F32)
            if dst is total:
                dst[at] = acc.astype(BF)
            else:
                dst[:, s] = acc.astype(BF)

    def flows(arr, n):
        zz = 3 - n

        @pl.when(z < zz)
        def _():
            along(arr, zz, from_left, act_left, 2, z > 0)

        @pl.when(z > n)
        def _():
            along(arr, n, from_right, act_right, -2, z < 3)

    def each(n, body):
        def step(i, _):
            body(i)
            return 0

        lax.fori_loop(0, n, step, 0)

    flows(0, 0)
    flows(1, 0)

    tx_copy(1).wait()
    x_copies[0].wait_recv()

    def add_lo(i):
        for h in range(2):
            xs_lo[i, h] = (tx1[i, h].astype(F32) + xa[i, h].astype(F32)).astype(BF)

    each(HALF, add_lo)
    x_copies[4].start()
    tx_copy(0).wait()
    x_copies[1].wait_recv()

    def add_hi(i):
        for h in range(2):
            xs_hi[i, h] = (tx0[HALF + i, h].astype(F32) + xb[i, h].astype(F32)).astype(BF)

    each(HALF, add_hi)
    x_copies[5].start()
    flows(0, 1)
    flows(1, 1)

    tx_copy(2).wait()
    for n in (2, 3, 4, 5):
        x_copies[n].wait_recv()

    def x_final(i):
        for h in range(2):
            v = tx2[i, h].astype(F32) + xl[i, h].astype(F32) + xr[i, h].astype(F32)
            for q in range(4):
                yb[q, i, h] = v[4 * q : 4 * q + 4].astype(BF)

    each(SLOTS, x_final)
    py, my = {"dp": yp}, {"dp": ym}
    yo, yf, yw = (y + 2) % 4, (y + 1) % 4, (y + 3) % 4
    y_copies = [
        remote(yb.at[yo, lo], ya, y_send.at[0], y_recv.at[0], py),
        remote(yb.at[yo, hi], yc, y_send.at[1], y_recv.at[1], my),
        remote(yb.at[yf, hi], yl.at[hi], y_send.at[2], y_recv.at[2], py),
        remote(yb.at[yw, lo], yr.at[lo], y_send.at[3], y_recv.at[3], my),
        remote(ys_lo, yl.at[lo], y_send.at[4], y_recv.at[4], py),
        remote(ys_hi, yr.at[hi], y_send.at[5], y_recv.at[5], my),
    ]
    for n in range(4):
        y_copies[n].start()
    y_copies[0].wait_recv()

    def add_ylo(i):
        ys_lo[i] = (yb[yf, i].astype(F32) + ya[i].astype(F32)).astype(BF)

    each(HALF, add_ylo)
    y_copies[4].start()
    y_copies[1].wait_recv()

    def add_yhi(i):
        ys_hi[i] = (yb[yw, HALF + i].astype(F32) + yc[i].astype(F32)).astype(BF)

    each(HALF, add_yhi)
    y_copies[5].start()
    for n in (2, 3, 4, 5):
        y_copies[n].wait_recv()

    def y_final(i):
        def of(h):
            return yb[y, i, h].astype(F32) + yl[i, h].astype(F32) + yr[i, h].astype(F32)

        z_own[i] = of(zh)
        z_send[i] = of(1 - zh).astype(BF)

    each(SLOTS, y_final)
    z_copy = remote(z_send, z_in, z_sems.at[0], z_sems.at[1], {"dp": zo})
    z_copy.start()
    flows(0, 2)
    flows(1, 2)
    z_copy.wait_recv()

    def z_final(i):
        z_sum[i] = (z_own[i] + z_in[i].astype(F32)).astype(BF)

    each(SLOTS, z_final)
    for m in range(3):

        def expand(j, base):
            n = counts[m, j]
            for k in range(3):
                v = z_sum[jnp.minimum(base + k, SLOTS - 1)]
                w_out[m * 42 + j * 3 + k] = jnp.where(k < n, v, jnp.zeros_like(v))
            return base + n

        lax.fori_loop(0, BLOCKS, expand, jnp.int32(m * CAP))

    for arr in range(2):
        own_copy(arr, z).wait()
        mate_copy(arr, z).wait_recv()

        @pl.when(z > 0)
        def _():
            remote(
                total.at[arr, z], from_left.at[arr, z], act_send.at[arr, z], act_left.at[arr, z],
                {"tensor": t},
            ).wait_recv()

        @pl.when(z < 3)
        def _():
            remote(
                total.at[arr, z], from_right.at[arr, z], act_send.at[arr, z], act_right.at[arr, z],
                {"tensor": t},
            ).wait_recv()

    for arr in range(2):
        base = (own, mate_in)
        for has_left, has_right in ((False, True), (True, True), (True, False)):
            here = (z == 0) if not has_left else ((z == 3) if not has_right else (z > 0) & (z < 3))
            bufs = base + ((from_left,) if has_left else ()) + ((from_right,) if has_right else ())

            @pl.when(here)
            def _():
                chunks(outs[arr], bufs, arr, z)

    for arr in range(2):
        for zz in range(4):
            mate_copy(arr, zz).wait_send()

            @pl.when(z != zz)
            def _():
                remote(
                    total.at[arr, zz],
                    from_left.at[arr, zz],
                    act_send.at[arr, zz],
                    act_left.at[arr, zz],
                    {"tensor": t},
                ).wait_send()

    for copy in x_copies + y_copies + [z_copy]:
        copy.wait_send()


def scatter(counts, f, i, tg):
    act = pltpu.VMEM((2, 4, ROWS, WIDTH), BF)
    dma = pltpu.SemaphoreType.DMA
    return pl.pallas_call(
        scatter_kernel,
        name="scatter",
        out_shape=(
            jax.ShapeDtypeStruct((ROWS, WIDTH), BF),
            jax.ShapeDtypeStruct((ROWS, WIDTH), BF),
            jax.ShapeDtypeStruct((3 * 42, 4, TILE), BF),
        ),
        in_specs=[SM, ANY, ANY, ANY],
        out_specs=(VM, VM, VM),
        scratch_shapes=[act] * 5
        + [pltpu.VMEM((SLOTS, 2, 16, TILE), BF)] * 3
        + [pltpu.VMEM((HALF, 2, 16, TILE), BF)] * 4
        + [pltpu.VMEM((SLOTS, 2, 16, TILE), BF)] * 2
        + [pltpu.VMEM((4, SLOTS, 2, 4, TILE), BF)]
        + [pltpu.VMEM((HALF, 2, 4, TILE), BF)] * 4
        + [pltpu.VMEM((SLOTS, 2, 4, TILE), BF)] * 2
        + [pltpu.VMEM((SLOTS, 4, TILE), F32)]
        + [pltpu.VMEM((SLOTS, 4, TILE), BF)] * 3
        + [dma((2, 4))] * 6
        + [dma((3,)), dma((6,)), dma((6,)), dma((6,)), dma((6,)), dma((2,))],
        compiler_params=pltpu.CompilerParams(
            collective_id=1, has_side_effects=True, vmem_limit_bytes=56 * 1024 * 1024
        ),
    )(counts, f, i, tg)


def shards(tokens, out_grad, weight_tiles, tile_counts, tile_rows):
    scale = 1.0 / math.sqrt(8192)
    tiles = weight_tiles.transpose(1, 2, 3, 0, 4).reshape(126, 4, TILE)
    rows = tile_rows.transpose(0, 2, 1).reshape(9, BLOCKS)
    x, g, w = gather(tile_counts, tokens, out_grad, tiles)
    f, i, tg = compute(tile_counts, rows, x, g, w.reshape(SLOTS, TILE, TILE), scale)
    f, i, tg = scatter(tile_counts, f, i, tg.reshape(SLOTS, 2, 4, 16, TILE))
    tile_grad = tg.reshape(3, BLOCKS, 3, 4, TILE).transpose(3, 0, 1, 2, 4)
    return (f, i, tile_grad)


def solution(mesh):
    return jax.shard_map(
        shards,
        mesh=mesh,
        in_specs=(
            P(("dp", "tensor"), None),
            P(("dp", "tensor"), None),
            P("dp", None, "tensor", None, None),
            P(None, "tensor"),
            P(None, "tensor", None),
        ),
        out_specs=(
            P(("dp", "tensor"), None),
            P(("dp", "tensor"), None),
            P("dp", None, "tensor", None, None),
        ),
        check_vma=False,
    )
```

time: 631 us -> 154 us (0.24)
  the two profiles are of different devices: /device:TPU:24 before, /device:TPU:32 now
where the time goes in v1:
time: 154 us; the launch traced here: 153 us
  Pallas kernels  146 us (95%)
  local copies, waits for them, and re-layouts  6.23 us (4%)
    pallas_call x1, Pallas kernels, scatter(): pl.pallas_call(scatter_kernel, name='scatter', out_shape=(jax.ShapeDtypeS...  74.9 us
    pallas_call x1, Pallas kernels, gather(): pl.pallas_call(gather_kernel, name='gather', out_shape=(jax.ShapeDtypeStr...  48.7 us
    pallas_call x1, Pallas kernels, compute(): pl.pallas_call(functools.partial(block_kernel, scale), name='blocks', out...  22.7 us
    unnamed x3, local copies, waits for them, and re-layouts  4.94 us

profile of v1, /device:TPU:32, one launch (start us, length us, event | category | flops | bytes accessed | tf_op | source)
XLA Modules:
  0.0 153.2 jit_solution(14581880100108034385)
XLA Ops:
  0.6 1.3 reshape.21.rows
  1.9 48.7 %gather.1 = (bf16[256,4096]{1,0:T(8,128)(2,1)}, bf16[256,4096]{1,0:T(8,128)(2,1)}, bf16[84,32,4,128]{3,2,1,0:T(4,128)(2,1)}) custom-call(s32[3,14]{1,0:T(4,128)} %counts.5, bf16[32,4096]{1,0:T(8,128)(2,1)} %x_in.1, bf16[32,4096]{1,0:T(8,128)(2,1)} %g_in.1, bf16[126,4,128]{2,1,0:T(4,128)(2,1)} %bitcast.11), custom_call_target="tpu_custom_call" | custom-call | tf_op jit(solution)/shard_map/gather/pallas_call | solution.py:247
  50.6 22.7 %blocks.1 = (bf16[256,4096]{1,0:T(8,128)(2,1)}, bf16[256,4096]{1,0:T(8,128)(2,1)}, bf16[84,128,128]{2,1,0:T(8,128)(2,1)}) custom-call(s32[3,14]{1,0:T(4,128)} %counts.5, s32[9,14]{1,0:T(8,128)} %reshape.21.rows, bf16[256,4096]{1,0:T(8,128)(2,1)} %get-tuple-element.12.x, bf16[256,4096]{1,0:T(8,128)(2,1)} %get-tuple-element.13.g, bf16[84,128,128]{2,1,0:T(8,128)(2,1)} %bitcast.10), custom_call_target="tpu_custom_call" | custom-call | tf_op jit(solution)/shard_map/blocks/pallas_call | solution.py:344
  73.3 74.9 %scatter.1 = (bf16[32,4096]{1,0:T(8,128)(2,1)}, bf16[32,4096]{1,0:T(8,128)(2,1)}, bf16[126,4,128]{2,1,0:T(4,128)(2,1)}) custom-call(s32[3,14]{1,0:T(4,128)} %counts.5, bf16[256,4096]{1,0:T(8,128)(2,1)} %get-tuple-element.15.f_in, bf16[256,4096]{1,0:T(8,128)(2,1)} %get-tuple-element.16.i_in, bf16[84,2,4,16,128]{4,3,2,1,0:T(8,128)(2,1)} %bitcast.9), custom_call_target="tpu_custom_call" | custom-call | tf_op jit(solution)/shard_map/scatter/pallas_call | solution.py:656
  148.2 1.7 %copy.11 = bf16[32,4096]{1,0:T(8,128)(2,1)} copy(bf16[32,4096]{1,0:T(8,128)(2,1)} %get-tuple-element.24) | data formatting | bytes 524288
  149.9 1.7 %copy.12 = bf16[32,4096]{1,0:T(8,128)(2,1)} copy(bf16[32,4096]{1,0:T(8,128)(2,1)} %get-tuple-element.25) | data formatting | bytes 524288
  151.6 1.6 %copy.13 = bf16[4,3,14,3,128]{4,0,3,2,1:T(4,128)(2,1)} copy(bf16[4,3,14,3,128]{4,0,3,2,1:T(4,128)(2,1)} %bitcast.12) | data formatting | bytes 258048

commit v2 on v1

--- a/solution.py
+++ b/solution.py
@@ -288,7 +288,7 @@
             where.append([])
             for k in range(3):
                 on = k < n
-                r = rows[m * 3 + k, j]
+                r = rows[m, k, j]
                 at = m * CAP + offsets[m] + k
                 tile = w[jnp.minimum(at, SLOTS - 1)]
                 if k:
@@ -357,7 +357,6 @@
 
 
 def scatter_kernel(
-    counts,
     f_in,
     i_in,
     tg,
@@ -388,7 +387,6 @@
     z_own,
     z_send,
     z_in,
-    z_sum,
     act_local,
     act_mate_s,
     act_mate_r,
@@ -460,26 +458,19 @@
     for n in range(3):
         tx_copy(n).start()
 
-    def along(arr, zz, buf, sems, way, has):
+    def along(arr, zz, buf, sems, way, first):
         own_copy(arr, zz).wait()
         mate_copy(arr, zz).wait_recv()
-
-        @pl.when(has)
-        def _():
-            remote(
-                total.at[arr, zz], buf.at[arr, zz], act_send.at[arr, zz], sems.at[arr, zz],
-                {"tensor": t},
-            ).wait_recv()
-            chunks(total, (own, mate_in, buf), arr, zz)
-
-        @pl.when(jnp.logical_not(has))
-        def _():
-            chunks(total, (own, mate_in), arr, zz)
-
-        remote(
+        hop = remote(
             total.at[arr, zz], buf.at[arr, zz], act_send.at[arr, zz], sems.at[arr, zz],
             {"tensor": t + way},
-        ).start()
+        )
+        if first:
+            chunks(total, (own, mate_in), arr, zz)
+        else:
+            hop.wait_recv()
+            chunks(total, (own, mate_in, buf), arr, zz)
+        hop.start()
 
     def chunks(dst, srcs, *lead):
         for n in range(0, WIDTH, 512):
@@ -493,16 +484,60 @@
             else:
                 dst[:, s] = acc.astype(BF)
 
-    def flows(arr, n):
-        zz = 3 - n
-
-        @pl.when(z < zz)
-        def _():
-            along(arr, zz, from_left, act_left, 2, z > 0)
-
-        @pl.when(z > n)
-        def _():
-            along(arr, n, from_right, act_right, -2, z < 3)
+    def ends():
+        @pl.when(z == 0)
+        def _():
+            for zz in (3, 2, 1):
+                for arr in range(2):
+                    along(arr, zz, from_left, act_left, 2, True)
+
+        @pl.when(z == 3)
+        def _():
+            for zz in (0, 1, 2):
+                for arr in range(2):
+                    along(arr, zz, from_right, act_right, -2, True)
+
+    def middle(arr, n):
+        @pl.when(z == 1)
+        def _():
+            if n < 2:
+                along(arr, 3 - n, from_left, act_left, 2, False)
+            else:
+                along(arr, 0, from_right, act_right, -2, False)
+
+        @pl.when(z == 2)
+        def _():
+            if n < 2:
+                along(arr, n, from_right, act_right, -2, False)
+            else:
+                along(arr, 3, from_left, act_left, 2, False)
+
+    def final(arr):
+        own_copy(arr, z).wait()
+        mate_copy(arr, z).wait_recv()
+
+        @pl.when(z > 0)
+        def _():
+            remote(
+                total.at[arr, z], from_left.at[arr, z], act_send.at[arr, z], act_left.at[arr, z],
+                {"tensor": t},
+            ).wait_recv()
+
+        @pl.when(z < 3)
+        def _():
+            remote(
+                total.at[arr, z], from_right.at[arr, z], act_send.at[arr, z], act_right.at[arr, z],
+                {"tensor": t},
+            ).wait_recv()
+
+        base = (own, mate_in)
+        for has_left, has_right in ((False, True), (True, True), (True, False)):
+            here = (z == 0) if not has_left else ((z == 3) if not has_right else (z > 0) & (z < 3))
+            bufs = base + ((from_left,) if has_left else ()) + ((from_right,) if has_right else ())
+
+            @pl.when(here)
+            def _():
+                chunks(outs[arr], bufs, arr, z)
 
     def each(n, body):
         def step(i, _):
@@ -511,8 +546,8 @@
 
         lax.fori_loop(0, n, step, 0)
 
-    flows(0, 0)
-    flows(1, 0)
+    ends()
+    middle(0, 0)
 
     tx_copy(1).wait()
     x_copies[0].wait_recv()
@@ -532,8 +567,10 @@
 
     each(HALF, add_hi)
     x_copies[5].start()
-    flows(0, 1)
-    flows(1, 1)
+    middle(1, 0)
+    middle(0, 2)
+    middle(0, 1)
+    middle(1, 2)
 
     tx_copy(2).wait()
     for n in (2, 3, 4, 5):
@@ -558,6 +595,7 @@
     ]
     for n in range(4):
         y_copies[n].start()
+    middle(1, 1)
     y_copies[0].wait_recv()
 
     def add_ylo(i):
@@ -585,53 +623,14 @@
     each(SLOTS, y_final)
     z_copy = remote(z_send, z_in, z_sems.at[0], z_sems.at[1], {"dp": zo})
     z_copy.start()
-    flows(0, 2)
-    flows(1, 2)
+    final(0)
+    final(1)
     z_copy.wait_recv()
 
     def z_final(i):
-        z_sum[i] = (z_own[i] + z_in[i].astype(F32)).astype(BF)
+        w_out[i] = (z_own[i] + z_in[i].astype(F32)).astype(BF)
 
     each(SLOTS, z_final)
-    for m in range(3):
-
-        def expand(j, base):
-            n = counts[m, j]
-            for k in range(3):
-                v = z_sum[jnp.minimum(base + k, SLOTS - 1)]
-                w_out[m * 42 + j * 3 + k] = jnp.where(k < n, v, jnp.zeros_like(v))
-            return base + n
-
-        lax.fori_loop(0, BLOCKS, expand, jnp.int32(m * CAP))
-
-    for arr in range(2):
-        own_copy(arr, z).wait()
-        mate_copy(arr, z).wait_recv()
-
-        @pl.when(z > 0)
-        def _():
-            remote(
-                total.at[arr, z], from_left.at[arr, z], act_send.at[arr, z], act_left.at[arr, z],
-                {"tensor": t},
-            ).wait_recv()
-
-        @pl.when(z < 3)
-        def _():
-            remote(
-                total.at[arr, z], from_right.at[arr, z], act_send.at[arr, z], act_right.at[arr, z],
-                {"tensor": t},
-            ).wait_recv()
-
-    for arr in range(2):
-        base = (own, mate_in)
-        for has_left, has_right in ((False, True), (True, True), (True, False)):
-            here = (z == 0) if not has_left else ((z == 3) if not has_right else (z > 0) & (z < 3))
-            bufs = base + ((from_left,) if has_left else ()) + ((from_right,) if has_right else ())
-
-            @pl.when(here)
-            def _():
-                chunks(outs[arr], bufs, arr, z)
-
     for arr in range(2):
         for zz in range(4):
             mate_copy(arr, zz).wait_send()
@@ -650,7 +649,7 @@
         copy.wait_send()
 
 
-def scatter(counts, f, i, tg):
+def scatter(f, i, tg):
     act = pltpu.VMEM((2, 4, ROWS, WIDTH), BF)
     dma = pltpu.SemaphoreType.DMA
     return pl.pallas_call(
@@ -659,9 +658,9 @@
         out_shape=(
             jax.ShapeDtypeStruct((ROWS, WIDTH), BF),
             jax.ShapeDtypeStruct((ROWS, WIDTH), BF),
-            jax.ShapeDtypeStruct((3 * 42, 4, TILE), BF),
+            jax.ShapeDtypeStruct((SLOTS, 4, TILE), BF),
         ),
-        in_specs=[SM, ANY, ANY, ANY],
+        in_specs=[ANY, ANY, ANY],
         out_specs=(VM, VM, VM),
         scratch_shapes=[act] * 5
         + [pltpu.VMEM((SLOTS, 2, 16, TILE), BF)] * 3
@@ -671,22 +670,52 @@
         + [pltpu.VMEM((HALF, 2, 4, TILE), BF)] * 4
         + [pltpu.VMEM((SLOTS, 2, 4, TILE), BF)] * 2
         + [pltpu.VMEM((SLOTS, 4, TILE), F32)]
-        + [pltpu.VMEM((SLOTS, 4, TILE), BF)] * 3
+        + [pltpu.VMEM((SLOTS, 4, TILE), BF)] * 2
         + [dma((2, 4))] * 6
         + [dma((3,)), dma((6,)), dma((6,)), dma((6,)), dma((6,)), dma((2,))],
         compiler_params=pltpu.CompilerParams(
             collective_id=1, has_side_effects=True, vmem_limit_bytes=56 * 1024 * 1024
         ),
+    )(f, i, tg)
+
+
+def finish_kernel(counts, f_in, i_in, w_in, f_out, i_out, w_out):
+    f_out[...] = f_in[...]
+    i_out[...] = i_in[...]
+    for m in range(3):
+
+        def expand(j, base):
+            n = counts[m, j]
+            for k in range(3):
+                v = w_in[jnp.minimum(base + k, SLOTS - 1)]
+                w_out[m * 42 + j * 3 + k] = jnp.where(k < n, v, jnp.zeros_like(v))
+            return base + n
+
+        lax.fori_loop(0, BLOCKS, expand, jnp.int32(m * CAP))
+
+
+def finish(counts, f, i, tg):
+    return pl.pallas_call(
+        finish_kernel,
+        name="finish",
+        out_shape=(
+            jax.ShapeDtypeStruct(f.shape, BF),
+            jax.ShapeDtypeStruct(i.shape, BF),
+            jax.ShapeDtypeStruct((3 * 42, 4, TILE), BF),
+        ),
+        in_specs=[SM, VM, VM, VM],
+        out_specs=(VM, VM, VM),
     )(counts, f, i, tg)
 
 
 def shards(tokens, out_grad, weight_tiles, tile_counts, tile_rows):
     scale = 1.0 / math.sqrt(8192)
     tiles = weight_tiles.transpose(1, 2, 3, 0, 4).reshape(126, 4, TILE)
-    rows = tile_rows.transpose(0, 2, 1).reshape(9, BLOCKS)
+    rows = tile_rows.transpose(0, 2, 1)
     x, g, w = gather(tile_counts, tokens, out_grad, tiles)
     f, i, tg = compute(tile_counts, rows, x, g, w.reshape(SLOTS, TILE, TILE), scale)
-    f, i, tg = scatter(tile_counts, f, i, tg.reshape(SLOTS, 2, 4, 16, TILE))
+    f, i, tg = scatter(f, i, tg.reshape(SLOTS, 2, 4, 16, TILE))
+    f, i, tg = finish(tile_counts, f, i, tg)
     tile_grad = tg.reshape(3, BLOCKS, 3, 4, TILE).transpose(3, 0, 1, 2, 4)
     return (f, i, tile_grad)
 

time: 154 us -> 127 us (0.82)
  the two profiles are of different devices: /device:TPU:32 before, /device:TPU:24 now
where the time goes in v2:
time: 127 us
  Pallas kernels  127 us (100%)
    pallas_call x1, Pallas kernels, gather(): pl.pallas_call(gather_kernel, name='gather', out_shape=(jax.ShapeDtypeStr...  52.7 us
    pallas_call x1, Pallas kernels, scatter(): pl.pallas_call(scatter_kernel, name='scatter', out_shape=(jax.ShapeDtypeS...  48.7 us
    pallas_call x1, Pallas kernels, compute(): pl.pallas_call(functools.partial(block_kernel, scale), name='blocks', out...  22.7 us

profile of v2, /device:TPU:24, one launch (start us, length us, event | category | flops | bytes accessed | tf_op | source)
XLA Modules:
  0.0 127.3 jit_solution(666918447437040579)
XLA Ops:
  0.6 52.7 %gather.1 = (bf16[256,4096]{1,0:T(8,128)(2,1)}, bf16[256,4096]{1,0:T(8,128)(2,1)}, bf16[84,32,4,128]{3,2,1,0:T(4,128)(2,1)}) custom-call(s32[3,14]{1,0:T(4,128)} %counts.5, bf16[32,4096]{1,0:T(8,128)(2,1)} %x_in.1, bf16[32,4096]{1,0:T(8,128)(2,1)} %g_in.1, bf16[126,4,128]{2,1,0:T(4,128)(2,1)} %bitcast.11), custom_call_target="tpu_custom_call" | custom-call | tf_op jit(solution)/shard_map/gather/pallas_call | solution.py:247
  53.4 22.7 %blocks.1 = (bf16[256,4096]{1,0:T(8,128)(2,1)}, bf16[256,4096]{1,0:T(8,128)(2,1)}, bf16[84,128,128]{2,1,0:T(8,128)(2,1)}) custom-call(s32[3,14]{1,0:T(4,128)} %counts.5, s32[3,3,14]{2,1,0:T(4,128)} %bitcast.12, bf16[256,4096]{1,0:T(8,128)(2,1)} %get-tuple-element.15.x, bf16[256,4096]{1,0:T(8,128)(2,1)} %get-tuple-element.16.g, bf16[84,128,128]{2,1,0:T(8,128)(2,1)} %bitcast.10), custom_call_target="tpu_custom_call" | custom-call | tf_op jit(solution)/shard_map/blocks/pallas_call | solution.py:344
  76.0 48.7 %scatter.1 = (bf16[32,4096]{1,0:T(8,128)(2,1)}, bf16[32,4096]{1,0:T(8,128)(2,1)}, bf16[84,4,128]{2,1,0:T(4,128)(2,1)}) custom-call(bf16[256,4096]{1,0:T(8,128)(2,1)} %get-tuple-element.18.f_in, bf16[256,4096]{1,0:T(8,128)(2,1)} %get-tuple-element.19.i_in, bf16[84,2,4,16,128]{4,3,2,1,0:T(8,128)(2,1)} %bitcast.9), custom_call_target="tpu_custom_call" | custom-call | tf_op jit(solution)/shard_map/scatter/pallas_call | solution.py:655
  124.8 2.5 %finish.1 = (bf16[32,4096]{1,0:T(8,128)(2,1)}, bf16[32,4096]{1,0:T(8,128)(2,1)}, bf16[126,4,128]{2,1,0:T(4,128)(2,1)}) custom-call(s32[3,14]{1,0:T(4,128)} %counts.5, bf16[32,4096]{1,0:T(8,128)(2,1)} %get-tuple-element.21.f_in, bf16[32,4096]{1,0:T(8,128)(2,1)} %get-tuple-element.22.i_in, bf16[84,4,128]{2,1,0:T(4,128)(2,1)} %get-tuple-element.23.w_in), custom_call_target="tpu_custom_call" | custom-call | tf_op jit(solution)/shard_map/finish/pallas_call | solution.py:698

commit v3 on v2

--- a/solution.py
+++ b/solution.py
@@ -248,9 +248,9 @@
         gather_kernel,
         name="gather",
         out_shape=(
-            jax.ShapeDtypeStruct((8 * ROWS, WIDTH), BF),
-            jax.ShapeDtypeStruct((8 * ROWS, WIDTH), BF),
-            jax.ShapeDtypeStruct((SLOTS, 32, 4, TILE), BF),
+            pltpu.VMEM((8 * ROWS, WIDTH), BF),
+            pltpu.VMEM((8 * ROWS, WIDTH), BF),
+            pltpu.VMEM((SLOTS, 32, 4, TILE), BF),
         ),
         in_specs=[SM, ANY, ANY, VM],
         out_specs=(ANY, ANY, ANY),
@@ -262,7 +262,9 @@
             pltpu.SemaphoreType.DMA((32, 2)),
             pltpu.SemaphoreType.DMA((3,)),
         ],
-        compiler_params=pltpu.CompilerParams(collective_id=0, has_side_effects=True),
+        compiler_params=pltpu.CompilerParams(
+            collective_id=0, has_side_effects=True, vmem_limit_bytes=4 * 1024 * 1024
+        ),
     )(counts, tokens, out_grad, tiles)
 
 
@@ -345,14 +347,14 @@
         functools.partial(block_kernel, scale),
         name="blocks",
         out_shape=(
-            jax.ShapeDtypeStruct(x.shape, BF),
-            jax.ShapeDtypeStruct(x.shape, BF),
-            jax.ShapeDtypeStruct((SLOTS, TILE, TILE), BF),
+            pltpu.VMEM(x.shape, BF),
+            pltpu.VMEM(x.shape, BF),
+            pltpu.VMEM((SLOTS, TILE, TILE), BF),
         ),
         in_specs=[SM, SM, VM, VM, VM],
         out_specs=(VM, VM, VM),
         scratch_shapes=[pltpu.VMEM(x.shape, F32), pltpu.VMEM(x.shape, F32)],
-        compiler_params=pltpu.CompilerParams(vmem_limit_bytes=56 * 1024 * 1024),
+        compiler_params=pltpu.CompilerParams(vmem_limit_bytes=32 * 1024 * 1024),
     )(counts, rows, x, g, w)
 
 
@@ -674,7 +676,7 @@
         + [dma((2, 4))] * 6
         + [dma((3,)), dma((6,)), dma((6,)), dma((6,)), dma((6,)), dma((2,))],
         compiler_params=pltpu.CompilerParams(
-            collective_id=1, has_side_effects=True, vmem_limit_bytes=56 * 1024 * 1024
+            collective_id=1, has_side_effects=True, vmem_limit_bytes=36 * 1024 * 1024
         ),
     )(f, i, tg)
 
@@ -705,6 +707,7 @@
         ),
         in_specs=[SM, VM, VM, VM],
         out_specs=(VM, VM, VM),
+        compiler_params=pltpu.CompilerParams(vmem_limit_bytes=4 * 1024 * 1024),
     )(counts, f, i, tg)
 
 
@@ -712,6 +715,10 @@
     scale = 1.0 / math.sqrt(8192)
     tiles = weight_tiles.transpose(1, 2, 3, 0, 4).reshape(126, 4, TILE)
     rows = tile_rows.transpose(0, 2, 1)
+    tokens, out_grad, tiles, tile_counts, rows = (
+        pltpu.with_memory_space_constraint(v, pltpu.HBM)
+        for v in (tokens, out_grad, tiles, tile_counts, rows)
+    )
     x, g, w = gather(tile_counts, tokens, out_grad, tiles)
     f, i, tg = compute(tile_counts, rows, x, g, w.reshape(SLOTS, TILE, TILE), scale)
     f, i, tg = scatter(f, i, tg.reshape(SLOTS, 2, 4, 16, TILE))

time: 127 us -> 121 us (0.953)
  Pallas kernels: 127 us -> 120 us
    pallas_call x1, Pallas kernels: 22.7 us -> 18.1 us  [compute(): pl.pallas_call(functools.partial(block_kernel, scale), name='blocks', out...]
where the time goes in v3:
time: 121 us
  Pallas kernels  120 us (99%)
    pallas_call x1, Pallas kernels, gather(): pl.pallas_call(gather_kernel, name='gather', out_shape=(pltpu.VMEM((8 * R...  52.3 us
    pallas_call x1, Pallas kernels, scatter(): pl.pallas_call(scatter_kernel, name='scatter', out_shape=(jax.ShapeDtypeS...  48 us
    pallas_call x1, Pallas kernels, compute(): pl.pallas_call(functools.partial(block_kernel, scale), name='blocks', out...  18.1 us

profile of v3, /device:TPU:24, one launch (start us, length us, event | category | flops | bytes accessed | tf_op | source)
XLA Modules:
  0.0 121.1 jit_solution(353296610458693491)
XLA Ops:
  0.6 52.3 %gather.1 = (bf16[256,4096]{1,0:T(8,128)(2,1)S(1)}, bf16[256,4096]{1,0:T(8,128)(2,1)S(1)}, bf16[84,32,4,128]{3,2,1,0:T(4,128)(2,1)S(1)}) custom-call(s32[3,14]{1,0:T(4,128)} %counts.5, bf16[32,4096]{1,0:T(8,128)(2,1)} %x_in.1, bf16[32,4096]{1,0:T(8,128)(2,1)} %g_in.1, bf16[126,4,128]{2,1,0:T(4,128)(2,1)} %bitcast.11), custom_call_target="tpu_custom_call" | custom-call | tf_op jit(solution)/shard_map/gather/pallas_call | solution.py:247
  52.9 18.1 %blocks.1 = (bf16[256,4096]{1,0:T(8,128)(2,1)S(1)}, bf16[256,4096]{1,0:T(8,128)(2,1)S(1)}, bf16[84,128,128]{2,1,0:T(8,128)(2,1)S(1)}) custom-call(s32[3,14]{1,0:T(4,128)} %counts.5, s32[3,3,14]{2,1,0:T(4,128)} %bitcast.12, bf16[256,4096]{1,0:T(8,128)(2,1)S(1)} %get-tuple-element.15.x, bf16[256,4096]{1,0:T(8,128)(2,1)S(1)} %get-tuple-element.16.g, ...), custom_call_target="tpu_custom_call" | custom-call | tf_op jit(solution)/shard_map/blocks/pallas_call | solution.py:346
  71.0 48.0 %scatter.1 = (bf16[32,4096]{1,0:T(8,128)(2,1)S(1)}, bf16[32,4096]{1,0:T(8,128)(2,1)S(1)}, bf16[84,4,128]{2,1,0:T(4,128)(2,1)S(1)}) custom-call(bf16[256,4096]{1,0:T(8,128)(2,1)S(1)} %get-tuple-element.18.f_in, bf16[256,4096]{1,0:T(8,128)(2,1)S(1)} %get-tuple-element.19.i_in, bf16[84,2,4,16,128]{4,3,2,1,0:T(8,128)(2,1)S(1)} %bitcast.9), custom_call_target="tpu_custom_call" | custom-call | tf_op jit(solution)/shard_map/scatter/pallas_call | solution.py:657
  119.0 2.1 %finish.1 = (bf16[32,4096]{1,0:T(8,128)(2,1)}, bf16[32,4096]{1,0:T(8,128)(2,1)}, bf16[126,4,128]{2,1,0:T(4,128)(2,1)}) custom-call(s32[3,14]{1,0:T(4,128)} %counts.5, bf16[32,4096]{1,0:T(8,128)(2,1)S(1)} %get-tuple-element.21.f_in, bf16[32,4096]{1,0:T(8,128)(2,1)S(1)} %get-tuple-element.22.i_in, bf16[84,4,128]{2,1,0:T(4,128)(2,1)S(1)} %get-tuple-element.23.w_in), custom_call_target="tpu_custom_call" | custom-call | tf_op jit(solution)/shard_map/finish/pallas_call | solution.py:700

commit v4 on v3

--- a/solution.py
+++ b/solution.py
@@ -322,22 +322,16 @@
             for k in range(3):
                 r, at = where[m][k]
 
-                def put():
-                    column(acc, r)[...] += wide[:, k * TILE : (k + 1) * TILE]
-                    part = (
-                        terms[k * TILE : (k + 1) * TILE]
-                        if m < 2
-                        else terms[:, k * TILE : (k + 1) * TILE]
-                    )
-                    tg[at] = part.astype(BF)
-
-                if k:
-                    pl.when(live[m][k])(put)
-                else:
-                    put()
+                column(acc, r)[...] += wide[:, k * TILE : (k + 1) * TILE]
+                part = (
+                    terms[k * TILE : (k + 1) * TILE]
+                    if m < 2
+                    else terms[:, k * TILE : (k + 1) * TILE]
+                )
+                tg[jnp.where(live[m][k], at, SLOTS) if k else at] = part.astype(BF)
         return tuple(offsets[m] + counts[m, j] for m in range(3))
 
-    lax.fori_loop(0, BLOCKS, step, (jnp.int32(0),) * 3)
+    lax.fori_loop(0, BLOCKS, step, (jnp.int32(0),) * 3, unroll=2)
     f_out[...] = acc_f[...].astype(BF)
     i_out[...] = acc_i[...].astype(BF)
 
@@ -349,7 +343,7 @@
         out_shape=(
             pltpu.VMEM(x.shape, BF),
             pltpu.VMEM(x.shape, BF),
-            pltpu.VMEM((SLOTS, TILE, TILE), BF),
+            pltpu.VMEM((SLOTS + 1, TILE, TILE), BF),
         ),
         in_specs=[SM, SM, VM, VM, VM],
         out_specs=(VM, VM, VM),
@@ -439,7 +433,7 @@
         )
 
     def tx_copy(n):
-        return pltpu.make_async_copy(tg.at[:, :, (x + (3, 1, 0)[n]) % 4], (tx0, tx1, tx2)[n], x_local.at[n])
+        return pltpu.make_async_copy(tg.at[pl.ds(0, SLOTS), :, (x + (3, 1, 0)[n]) % 4], (tx0, tx1, tx2)[n], x_local.at[n])
 
     px, mx = {"dp": xp}, {"dp": xm}
     opp, fwd, bwd = (x + 2) % 4, (x + 1) % 4, (x + 3) % 4
@@ -721,7 +715,7 @@
     )
     x, g, w = gather(tile_counts, tokens, out_grad, tiles)
     f, i, tg = compute(tile_counts, rows, x, g, w.reshape(SLOTS, TILE, TILE), scale)
-    f, i, tg = scatter(f, i, tg.reshape(SLOTS, 2, 4, 16, TILE))
+    f, i, tg = scatter(f, i, tg.reshape(SLOTS + 1, 2, 4, 16, TILE))
     f, i, tg = finish(tile_counts, f, i, tg)
     tile_grad = tg.reshape(3, BLOCKS, 3, 4, TILE).transpose(3, 0, 1, 2, 4)
     return (f, i, tile_grad)

time: 121 us -> 116 us (0.959)
  Pallas kernels: 120 us -> 115 us
    pallas_call x1, Pallas kernels: 18.1 us -> 12.5 us  [compute(): pl.pallas_call(functools.partial(block_kernel, scale), name='blocks', out...]
where the time goes in v4:
time: 116 us; the launch traced here: 115 us
  Pallas kernels  115 us (99%)
    pallas_call x1, Pallas kernels, gather(): pl.pallas_call(gather_kernel, name='gather', out_shape=(pltpu.VMEM((8 * R...  52.3 us
    pallas_call x1, Pallas kernels, scatter(): pl.pallas_call(scatter_kernel, name='scatter', out_shape=(jax.ShapeDtypeS...  47.8 us
    pallas_call x1, Pallas kernels, compute(): pl.pallas_call(functools.partial(block_kernel, scale), name='blocks', out...  12.5 us

profile of v4, /device:TPU:24, one launch (start us, length us, event | category | flops | bytes accessed | tf_op | source)
XLA Modules:
  0.0 115.4 jit_solution(9014417652608327079)
XLA Ops:
  0.6 52.3 %gather.1 = (bf16[256,4096]{1,0:T(8,128)(2,1)S(1)}, bf16[256,4096]{1,0:T(8,128)(2,1)S(1)}, bf16[84,32,4,128]{3,2,1,0:T(4,128)(2,1)S(1)}) custom-call(s32[3,14]{1,0:T(4,128)} %counts.5, bf16[32,4096]{1,0:T(8,128)(2,1)} %x_in.1, bf16[32,4096]{1,0:T(8,128)(2,1)} %g_in.1, bf16[126,4,128]{2,1,0:T(4,128)(2,1)} %bitcast.11), custom_call_target="tpu_custom_call" | custom-call | tf_op jit(solution)/shard_map/gather/pallas_call | solution.py:247
  52.9 12.5 %blocks.1 = (bf16[256,4096]{1,0:T(8,128)(2,1)S(1)}, bf16[256,4096]{1,0:T(8,128)(2,1)S(1)}, bf16[85,128,128]{2,1,0:T(8,128)(2,1)S(1)}) custom-call(s32[3,14]{1,0:T(4,128)} %counts.5, s32[3,3,14]{2,1,0:T(4,128)} %bitcast.12, bf16[256,4096]{1,0:T(8,128)(2,1)S(1)} %get-tuple-element.15.x, bf16[256,4096]{1,0:T(8,128)(2,1)S(1)} %get-tuple-element.16.g, ...), custom_call_target="tpu_custom_call" | custom-call | tf_op jit(solution)/shard_map/blocks/pallas_call | solution.py:340
  65.4 47.8 %scatter.1 = (bf16[32,4096]{1,0:T(8,128)(2,1)S(1)}, bf16[32,4096]{1,0:T(8,128)(2,1)S(1)}, bf16[84,4,128]{2,1,0:T(4,128)(2,1)S(1)}) custom-call(bf16[256,4096]{1,0:T(8,128)(2,1)S(1)} %get-tuple-element.18.f_in, bf16[256,4096]{1,0:T(8,128)(2,1)S(1)} %get-tuple-element.19.i_in, bf16[85,2,4,16,128]{4,3,2,1,0:T(8,128)(2,1)S(1)} %bitcast.9), custom_call_target="tpu_custom_call" | custom-call | tf_op jit(solution)/shard_map/scatter/pallas_call | solution.py:651
  113.2 2.1 %finish.1 = (bf16[32,4096]{1,0:T(8,128)(2,1)}, bf16[32,4096]{1,0:T(8,128)(2,1)}, bf16[126,4,128]{2,1,0:T(4,128)(2,1)}) custom-call(s32[3,14]{1,0:T(4,128)} %counts.5, bf16[32,4096]{1,0:T(8,128)(2,1)S(1)} %get-tuple-element.21.f_in, bf16[32,4096]{1,0:T(8,128)(2,1)S(1)} %get-tuple-element.22.i_in, bf16[84,4,128]{2,1,0:T(4,128)(2,1)S(1)} %get-tuple-element.23.w_in), custom_call_target="tpu_custom_call" | custom-call | tf_op jit(solution)/shard_map/finish/pallas_call | solution.py:694
